TPU v7x, 32 devices: a whole 2x2x4 slice. The times are simulated.
32 devices in a mesh: grp: 2 (over x), az: 8 (over z, y), ax: 2 (over core).
Axes of the slice: x: 2, y: 2, z: 4, core: 2. Of those that a mesh axis runs over, the one named last changes fastest.
Arguments:
- cavity_block: float32 [8, 96, 32, 256], P(None, 'grp', 'az', 'ax'), may hold values from -95 to 95
- shell_block: float32 [8, 6, 32, 256], P(None, None, 'az', 'ax'), may hold values from -95 to 95
- column_matrix: float32 [2, 48, 48], P('grp'), may hold values from -2 to 6, as said below
- shell_matrix: float32 [6, 6], replicated, may hold values from -2 to 6, as said below
- shifted_diagonal: float32 [96, 32, 256], P('grp', 'az', 'ax'), may hold values from 1.6 to 3
- shell_diagonal: float32 [6, 32, 256], P(None, 'az', 'ax'), may hold values from 1.6 to 3
- wet_area: float32 [32, 256], P('az', 'ax'), may hold values from 0.3 to 1.5
Outputs:
- cavity_solution: float32 [8, 96, 32, 256], P(None, 'grp', 'az', 'ax')
- cavity_residual: float32 [8, 96, 32, 256], P(None, 'grp', 'az', 'ax')
- shell_solution: float32 [8, 6, 32, 256], P(None, None, 'az', 'ax')
- shell_residual: float32 [8, 6, 32, 256], P(None, None, 'az', 'ax')
Inputs may be any that keep to these rules, and one draw needn't show every extreme that they name: `column_matrix`: each symmetric and positive definite. `shell_matrix`: symmetric and positive definite.
All inputs are finite; a program needn't handle non-finite values.
Results may differ from a plain program's by a relative error of at most 0.0015.
Values sent between devices are 32-bit elements; how exact they have to be, the bound alone decides.
No kernel may reach another device: no remote copies, remote signals or barrier semaphores. Data moves between devices by JAX's collectives and lax.ppermute only.
A program may use at most 128 MiB of HBM per device.

v0:
```python
import jax
import jax.numpy as jnp
from jax import lax
from jax.sharding import PartitionSpec as P

ITERS = 3
exact_mode = lax.Precision.HIGHEST


def swapped(block, axis, apart):
    count = lax.axis_size(axis)
    route = []
    for low in range(count):
        high = low | 1 << apart
        if high != low and high < count:
            route += [(low, high), (high, low)]
    return lax.ppermute(block, axis, route)


def extended(array, sides, width, wrap):
    for axis, dim in sides:
        peers, length = (lax.axis_size(axis), array.shape[dim])
        up = [(i, (i + 1) % peers) for i in range(peers if wrap else peers - 1)]
        down = [(j, i) for i, j in up]
        last = lax.slice_in_dim(array, length - width, length, axis=dim)
        first = lax.slice_in_dim(array, 0, width, axis=dim)
        before = lax.ppermute(last, axis, up)
        after = lax.ppermute(first, axis, down)
        array = jnp.concatenate([before, array, after], axis=dim)
    return array


def solve_posdef(gram_matrix, targets):
    factor = jnp.linalg.cholesky(gram_matrix)
    middle = lax.linalg.triangular_solve(factor, targets, left_side=True, lower=True)
    return lax.linalg.triangular_solve(factor, middle, left_side=True, lower=True, transpose_a=True)


def products(first_set, second_set):
    return jnp.einsum("vrax,wrax->vw", first_set, second_set, precision=exact_mode)


def combine(vector_set, mixing):
    return jnp.einsum("vrax,vw->wrax", vector_set, mixing, precision=exact_mode)


def column_part(vector_set, matrix):
    flat_set = vector_set.reshape(vector_set.shape[0], vector_set.shape[1], -1)
    mixed_set = jnp.einsum("rs,vsc->vrc", matrix, flat_set, precision=exact_mode)
    return mixed_set.reshape(vector_set.shape)


def coupled(result, vector_set, wet_area, layout):
    half, interface_row, outer_flag = layout
    iface_own = lax.dynamic_slice_in_dim(vector_set, interface_row, 1, 1)
    wall_own = vector_set[:, half - 1 : half]
    sent = jnp.concatenate([iface_own, wall_own], axis=1)
    received = swapped(sent, "grp", 0)
    result_row = lax.dynamic_slice_in_dim(result, interface_row, 1, 1)
    result = lax.dynamic_update_slice_in_dim(
        result, result_row - received[:, 0:1], interface_row, 1
    )
    wall = outer_flag * wall_own + (1.0 - outer_flag) * received[:, 1:2]
    shell_top = vector_set[:, half : half + 1]
    result = result.at[:, half - 1 : half].add(-outer_flag * wet_area * shell_top)
    result = result.at[:, half : half + 1].add(-wet_area * wall)
    return result


def apply_shallow(vector_set, matrix, diagonal_set, wet_area, layout):
    beside_all = extended(vector_set, (("az", 2),), 1, True)
    along = extended(vector_set, (("ax", 3),), 1, False)
    neighbours = beside_all[:, :, 2:] + beside_all[:, :, :-2] + along[..., 2:] + along[..., :-2]
    result = column_part(vector_set, matrix) + (4.0 + diagonal_set) * vector_set - neighbours
    return coupled(result, vector_set, wet_area, layout)


def per_device(
    cavity_block,
    shell_block,
    column_matrix,
    shell_matrix,
    shifted_diagonal,
    shell_diagonal,
    wet_area,
):
    group_index = lax.axis_index("grp")
    outer_flag = (group_index == 1).astype(jnp.float32)
    shell_share = 1.0 - outer_flag
    half = column_matrix.shape[1]
    shell_rows = shell_matrix.shape[0]
    interface_row = jnp.where(group_index == 1, 0, half - 1).astype(jnp.int32)
    layout = (half, interface_row, outer_flag)
    upper = jnp.concatenate([column_matrix[0], jnp.zeros((half, shell_rows), jnp.float32)], axis=1)
    lower = jnp.concatenate([jnp.zeros((shell_rows, half), jnp.float32), shell_matrix], axis=1)
    matrix = jnp.concatenate([upper, lower], axis=0)
    right_side = jnp.concatenate([cavity_block, shell_block], axis=1)
    diagonal_own = jnp.concatenate([shifted_diagonal, shell_diagonal], axis=0)

    def moments_local(first_set, second_set):
        cavity_part = products(first_set[:, :half], second_set[:, :half])
        return cavity_part + shell_share * products(first_set[:, half:], second_set[:, half:])

    residual = right_side
    direction = right_side
    solution = jnp.zeros_like(right_side)
    start_core = residual
    norms_now = lax.psum(moments_local(start_core, start_core), ("grp", "az", "ax"))
    for sweep in range(ITERS):
        image_set = apply_shallow(direction, matrix, diagonal_own, wet_area, layout)
        direction_core = direction
        residual_core = residual
        curvature, crossing, squares = lax.psum(
            (
                moments_local(direction_core, image_set),
                moments_local(image_set, residual_core),
                moments_local(image_set, image_set),
            ),
            ("grp", "az", "ax"),
        )
        step_mix = solve_posdef(curvature, norms_now)
        norms_next = norms_now - jnp.dot(step_mix.T, crossing, precision=exact_mode)
        norms_next = norms_next - jnp.dot(crossing.T, step_mix, precision=exact_mode)
        norms_next = norms_next + jnp.dot(
            jnp.dot(step_mix.T, squares, precision=exact_mode), step_mix, precision=exact_mode
        )
        solution = solution + combine(direction_core, step_mix)
        residual = residual - combine(image_set, step_mix)
        if sweep + 1 < ITERS:
            turn_mix = solve_posdef(norms_now, norms_next)
            direction = residual + combine(direction, turn_mix)
            norms_now = norms_next
    return (solution[:, :half], residual[:, :half], solution[:, half:], residual[:, half:])


def solution(mesh):
    return jax.shard_map(
        per_device,
        mesh=mesh,
        in_specs=(
            P(None, "grp", "az", "ax"),
            P(None, None, "az", "ax"),
            P("grp", None, None),
            P(),
            P("grp", "az", "ax"),
            P(None, "az", "ax"),
            P("az", "ax"),
        ),
        out_specs=(
            P(None, "grp", "az", "ax"),
            P(None, "grp", "az", "ax"),
            P(None, None, "az", "ax"),
            P(None, None, "az", "ax"),
        ),
        check_vma=False,
    )
```

profile of v0, /device:TPU:0, one launch (start us, length us, event | category | flops | bytes accessed | tf_op | source)
XLA Modules:
  0.0 250.7 jit_solution(17498085943303923312)
XLA Ops:
  0.6 2.5 fusion.124
  5.1 2.4 collective-permute-start.3
  10.0 2.3 collective-permute-start.1
  12.3 3.0 %collective-permute-start = (f32[8,54,1,128]{3,0,1,2:T(8,128)}, f32[8,54,1,128]{3,0,1,2:T(8,128)}, u32[]{:S(2)}, u32[]{:S(2)}) collective-permute-start(f32[8,54,1,128]{3,0,1,2:T(8,128)} %get-tuple-element.110), channel_id=1, source_target_pairs={{2,0},{4,2},{6,4},{8,6},{10,8},{12,10},{14,12},{0,14},{3,1},{5,3},... | collective-permute-start | bytes 663560 | tf_op jit(solution)/shard_map/ppermute | solution.py:28
  18.4 1.9 convolution_bitcast_fusion.3
  21.4 2.4 convolution_bitcast_fusion.2
  26.3 2.5 fusion.26
  31.0 1.9 convolution_bitcast_fusion.15
  32.9 1.8 convolution_bitcast_fusion.13
  35.7 38.6 %all-reduce.3 = (f32[8,8]{0,1:T(8,128)S(1)}, f32[8,8]{1,0:T(8,128)S(1)}, f32[8,8]{0,1:T(8,128)S(1)}, f32[8,8]{0,1:T(8,128)S(1)}) all-reduce(f32[8,8]{0,1:T(8,128)S(1)} %copy-done.18, f32[8,8]{1,0:T(8,128)S(1)} %bitcast.241, f32[8,8]{0,1:T(8,128)S(1)} %fusion.11, ...), channel_id=1, replica_groups=mesh['grp'=2,'az'=8,'ax'=2] {'grp','az','ax'}, use_global_device_ids=true, to_apply=%region_3.0 | all-reduce | flops 256 | bytes 2048 | tf_op jit(solution)/shard_map/psum | solution.py:108
  77.5 1.9 fusion.31
  88.4 2.1 copy.206
  90.6 1.9 collective-permute-start.8
  94.7 2.4 collective-permute-start.6
  97.1 2.4 collective-permute-start.5
  99.5 3.1 %convolution_bitcast_fusion.1 = f32[8,54,512]{2,1,0:T(8,128)} fusion(f32[8,54,512]{2,0,1:T(8,128)S(1)} %bitcast.235, f32[6,6]{1,0:T(8,128)S(1)} %copy-done.14, f32[48,48]{1,0:T(8,128)} %bitcast.238), kind=kOutput, calls=%fused_computation.1 | convolution fusion | flops 143341808 | bytes 1778832 | tf_op jit(solution)/shard_map/rs,vsc->vrc/dot_general | solution.py:49
  103.3 2.3 collective-permute-start.9
  112.0 2.5 fusion.22
  116.0 1.8 convolution_bitcast_fusion.11
  117.8 1.8 convolution_bitcast_fusion.9
  122.3 37.7 %all-reduce.2 = (f32[8,8]{0,1:T(8,128)S(1)}, f32[8,8]{0,1:T(8,128)}, f32[8,8]{0,1:T(8,128)}) all-reduce(f32[8,8]{0,1:T(8,128)S(1)} %fusion.7, f32[8,8]{0,1:T(8,128)S(1)} %fusion.5, f32[8,8]{0,1:T(8,128)S(1)} %fusion.3), channel_id=1, replica_groups=mesh['grp'=2,'az'=8,'ax'=2] {'grp','az','ax'}, use_global_device_ids=true, to_apply=%region_6.10 | all-reduce | flops 192 | bytes 1536 | tf_op jit(solution)/shard_map/psum | solution.py:113
  170.3 1.9 convolution_add_fusion.2
  172.1 2.2 copy.237
  174.4 2.0 collective-permute-start.13
  178.6 2.7 %collective-permute-start.11 = (f32[8,54,1,128]{3,0,1,2:T(8,128)}, f32[8,54,1,128]{3,0,1,2:T(8,128)S(1)}, u32[]{:S(2)}, u32[]{:S(2)}) collective-permute-start(f32[8,54,1,128]{3,0,1,2:T(8,128)} %get-tuple-element.101), channel_id=1, source_target_pairs={{0,2},{2,4},{4,6},{6,8},{8,10},{10,12},{12,14},{14,0},{1,3},{3,5},... | collective-permute-start | bytes 663560 | tf_op jit(solution)/shard_map/ppermute | solution.py:27
  181.3 2.1 collective-permute-start.10
  183.4 3.1 %convolution_bitcast_fusion = f32[8,54,512]{2,1,0:T(8,128)} fusion(f32[8,54,512]{2,0,1:T(8,128)S(1)} %bitcast.236, f32[6,6]{1,0:T(8,128)S(1)} %copy-done.14, f32[48,48]{1,0:T(8,128)} %bitcast.239), kind=kOutput, calls=%fused_computation | convolution fusion | flops 143341808 | bytes 1778832 | tf_op jit(solution)/shard_map/rs,vsc->vrc/dot_general | solution.py:49
  187.1 2.2 collective-permute-start.14
  192.7 1.8 collective-permute-done.10
  194.5 2.4 fusion.18
  198.5 1.8 convolution_bitcast_fusion.5
  200.5 38.7 %psum.63 = f32[8,8]{0,1:T(8,128)S(1)} all-reduce(f32[8,8]{0,1:T(8,128)S(1)} %fusion.1), channel_id=1, replica_groups=mesh['grp'=2,'az'=8,'ax'=2] {'grp','az','ax'}, use_global_device_ids=true, to_apply=%region_9.13 | all-reduce | flops 64 | bytes 512 | tf_op jit(solution)/shard_map/psum | solution.py:113
  (181 shorter events, 69.6 us)
Async XLA Ops:
  0.6 2.5 %copy-start.6 = (f32[8,6,4,128]{3,2,1,0:T(4,128)S(1)}, f32[8,6,4,128]{3,2,1,0:T(4,128)}, u32[]{:S(2)}) copy-start(f32[8,6,4,128]{3,2,1,0:T(4,128)} %param.25) | copy-start | bytes 294916
  5.1 19.4 %collective-permute-start.3 = (f32[8,54,4,1]{1,0,3,2:T(8,128)}, f32[8,54,4,1]{1,0,3,2:T(8,128)S(1)}, u32[]{:S(2)}, u32[]{:S(2)}) collective-permute-start(f32[8,54,4,1]{1,0,3,2:T(8,128)} %copy.166), channel_id=1, source_target_pairs={{0,1},{2,3},{4,5},{6,7},{8,9},{10,11},{12,13},{14,15},{16,17},{18,... | collective-permute-start | bytes 20744 | tf_op jit(solution)/shard_map/ppermute | solution.py:27
  7.5 10.9 %copy-start = (f32[8,48,4,128]{3,2,1,0:T(4,128)S(1)}, f32[8,48,4,128]{3,2,1,0:T(4,128)}, u32[]{:S(2)}) copy-start(f32[8,48,4,128]{3,2,1,0:T(4,128)} %param.24) | copy-start | bytes 2359300
  7.9 17.0 %collective-permute-start.2 = (f32[8,54,4,1]{1,0,3,2:T(8,128)S(1)}, f32[8,54,4,1]{1,0,3,2:T(8,128)S(1)}, u32[]{:S(2)}, u32[]{:S(2)}) collective-permute-start(f32[8,54,4,1]{1,0,3,2:T(8,128)S(1)} %copy.164), channel_id=1, source_target_pairs={{1,0},{3,2},{5,4},{7,6},{9,8},{11,10},{13,12},{15,14},{17,16},{19,... | collective-permute-start | bytes 20744 | tf_op jit(solution)/shard_map/ppermute | solution.py:28
  10.0 16.3 %collective-permute-start.1 = (f32[8,54,1,128]{3,0,1,2:T(8,128)}, f32[8,54,1,128]{3,0,1,2:T(8,128)}, u32[]{:S(2)}, u32[]{:S(2)}) collective-permute-start(f32[8,54,1,128]{3,0,1,2:T(8,128)} %get-tuple-element.111), channel_id=1, source_target_pairs={{0,2},{2,4},{4,6},{6,8},{8,10},{10,12},{12,14},{14,0},{1,3},{3,5},... | collective-permute-start | bytes 663560 | tf_op jit(solution)/shard_map/ppermute | solution.py:27
  12.3 14.0 %collective-permute-start = (f32[8,54,1,128]{3,0,1,2:T(8,128)}, f32[8,54,1,128]{3,0,1,2:T(8,128)}, u32[]{:S(2)}, u32[]{:S(2)}) collective-permute-start(f32[8,54,1,128]{3,0,1,2:T(8,128)} %get-tuple-element.110), channel_id=1, source_target_pairs={{2,0},{4,2},{6,4},{8,6},{10,8},{12,10},{14,12},{0,14},{3,1},{5,3},... | collective-permute-start | bytes 663560 | tf_op jit(solution)/shard_map/ppermute | solution.py:28
  16.7 12.1 %collective-permute-start.4 = (f32[8,2,4,128]{3,0,1,2:T(8,128)}, f32[8,2,4,128]{3,0,1,2:T(8,128)}, u32[]{:S(2)}, u32[]{:S(2)}) collective-permute-start(f32[8,2,4,128]{3,0,1,2:T(8,128)} %pad_maximum_fusion.12), channel_id=1, source_target_pairs={{0,16},{16,0},{1,17},{17,1},{2,18},{18,2},{3,19},{19,3},{4,20},{20... | collective-permute-start | bytes 98312 | tf_op jit(solution)/shard_map/ppermute | solution.py:17
  21.3 2.4 copy-start.21
  21.3 2.4 copy-start.11
  21.4 2.4 copy-start.19
  32.9 1.8 copy-start.7
  90.6 18.3 %collective-permute-start.8 = (f32[8,54,4,1]{1,0,3,2:T(8,128)}, f32[8,54,4,1]{1,0,3,2:T(8,128)}, u32[]{:S(2)}, u32[]{:S(2)}) collective-permute-start(f32[8,54,4,1]{1,0,3,2:T(8,128)} %copy.206), channel_id=1, source_target_pairs={{0,1},{2,3},{4,5},{6,7},{8,9},{10,11},{12,13},{14,15},{16,17},{18,... | collective-permute-start | bytes 20744 | tf_op jit(solution)/shard_map/ppermute | solution.py:27
  93.4 16.6 %collective-permute-start.7 = (f32[8,54,4,1]{1,0,3,2:T(8,128)}, f32[8,54,4,1]{1,0,3,2:T(8,128)S(1)}, u32[]{:S(2)}, u32[]{:S(2)}) collective-permute-start(f32[8,54,4,1]{1,0,3,2:T(8,128)} %copy.204), channel_id=1, source_target_pairs={{1,0},{3,2},{5,4},{7,6},{9,8},{11,10},{13,12},{15,14},{17,16},{19,... | collective-permute-start | bytes 20744 | tf_op jit(solution)/shard_map/ppermute | solution.py:28
  94.7 16.6 %collective-permute-start.6 = (f32[8,54,1,128]{3,0,1,2:T(8,128)}, f32[8,54,1,128]{3,0,1,2:T(8,128)S(1)}, u32[]{:S(2)}, u32[]{:S(2)}) collective-permute-start(f32[8,54,1,128]{3,0,1,2:T(8,128)} %get-tuple-element.107), channel_id=1, source_target_pairs={{0,2},{2,4},{4,6},{6,8},{8,10},{10,12},{12,14},{14,0},{1,3},{3,5},... | collective-permute-start | bytes 663560 | tf_op jit(solution)/shard_map/ppermute | solution.py:27
  97.1 14.9 %collective-permute-start.5 = (f32[8,54,1,128]{3,0,1,2:T(8,128)}, f32[8,54,1,128]{3,0,1,2:T(8,128)}, u32[]{:S(2)}, u32[]{:S(2)}) collective-permute-start(f32[8,54,1,128]{3,0,1,2:T(8,128)} %get-tuple-element.106), channel_id=1, source_target_pairs={{2,0},{4,2},{6,4},{8,6},{10,8},{12,10},{14,12},{0,14},{3,1},{5,3},... | collective-permute-start | bytes 663560 | tf_op jit(solution)/shard_map/ppermute | solution.py:28
  99.5 3.2 %copy-start.12 = (f32[8,1,4,128]{3,0,1,2:T(8,128)S(1)}, f32[8,1,4,128]{3,0,1,2:T(8,128)}, u32[]{:S(2)}) copy-start(f32[8,1,4,128]{3,0,1,2:T(8,128)} %get-tuple-element.104) | copy-start | bytes 49156
  99.5 3.2 %copy-start.13 = (f32[8,1,4,128]{3,0,1,2:T(8,128)S(1)}, f32[8,1,4,128]{3,0,1,2:T(8,128)}, u32[]{:S(2)}) copy-start(f32[8,1,4,128]{3,0,1,2:T(8,128)} %get-tuple-element.105) | copy-start | bytes 49156
  102.7 2.9 %copy-start.16 = (f32[8,8]{1,0:T(8,128)S(1)}, f32[8,8]{1,0:T(8,128)}, u32[]{:S(2)}) copy-start(f32[8,8]{1,0:T(8,128)} %copy.218) | copy-start | bytes 772
  103.3 11.2 %collective-permute-start.9 = (f32[8,2,4,128]{3,0,1,2:T(8,128)}, f32[8,2,4,128]{3,0,1,2:T(8,128)}, u32[]{:S(2)}, u32[]{:S(2)}) collective-permute-start(f32[8,2,4,128]{3,0,1,2:T(8,128)} %pad_maximum_fusion.13), channel_id=1, source_target_pairs={{0,16},{16,0},{1,17},{17,1},{2,18},{18,2},{3,19},{19,3},{4,20},{20... | collective-permute-start | bytes 98312 | tf_op jit(solution)/shard_map/ppermute | solution.py:17
  169.1 1.2 copy-start.2
  172.1 4.2 %copy-start.1 = (f32[8,54,4,1]{3,0,1,2:T(8,128)S(1)}, f32[8,54,4,1]{3,0,1,2:T(8,128)}, u32[]{:S(2)}) copy-start(f32[8,54,4,1]{3,0,1,2:T(8,128)} %get-tuple-element.102) | copy-start | bytes 20740
  174.4 15.0 %collective-permute-start.13 = (f32[8,54,4,1]{1,0,3,2:T(8,128)}, f32[8,54,4,1]{1,0,3,2:T(8,128)}, u32[]{:S(2)}, u32[]{:S(2)}) collective-permute-start(f32[8,54,4,1]{1,0,3,2:T(8,128)} %copy.237), channel_id=1, source_target_pairs={{0,1},{2,3},{4,5},{6,7},{8,9},{10,11},{12,13},{14,15},{16,17},{18,... | collective-permute-start | bytes 20744 | tf_op jit(solution)/shard_map/ppermute | solution.py:27
  177.3 13.2 %collective-permute-start.12 = (f32[8,54,4,1]{1,0,3,2:T(8,128)}, f32[8,54,4,1]{1,0,3,2:T(8,128)S(1)}, u32[]{:S(2)}, u32[]{:S(2)}) collective-permute-start(f32[8,54,4,1]{1,0,3,2:T(8,128)} %copy.235), channel_id=1, source_target_pairs={{1,0},{3,2},{5,4},{7,6},{9,8},{11,10},{13,12},{15,14},{17,16},{19,... | collective-permute-start | bytes 20744 | tf_op jit(solution)/shard_map/ppermute | solution.py:28
  178.6 13.4 %collective-permute-start.11 = (f32[8,54,1,128]{3,0,1,2:T(8,128)}, f32[8,54,1,128]{3,0,1,2:T(8,128)S(1)}, u32[]{:S(2)}, u32[]{:S(2)}) collective-permute-start(f32[8,54,1,128]{3,0,1,2:T(8,128)} %get-tuple-element.101), channel_id=1, source_target_pairs={{0,2},{2,4},{4,6},{6,8},{8,10},{10,12},{12,14},{14,0},{1,3},{3,5},... | collective-permute-start | bytes 663560 | tf_op jit(solution)/shard_map/ppermute | solution.py:27
  181.3 13.2 %collective-permute-start.10 = (f32[8,54,1,128]{3,0,1,2:T(8,128)}, f32[8,54,1,128]{3,0,1,2:T(8,128)}, u32[]{:S(2)}, u32[]{:S(2)}) collective-permute-start(f32[8,54,1,128]{3,0,1,2:T(8,128)} %get-tuple-element.100), channel_id=1, source_target_pairs={{2,0},{4,2},{6,4},{8,6},{10,8},{12,10},{14,12},{0,14},{3,1},{5,3},... | collective-permute-start | bytes 663560 | tf_op jit(solution)/shard_map/ppermute | solution.py:28
  187.1 9.8 %collective-permute-start.14 = (f32[8,2,4,128]{3,0,1,2:T(8,128)}, f32[8,2,4,128]{3,0,1,2:T(8,128)}, u32[]{:S(2)}, u32[]{:S(2)}) collective-permute-start(f32[8,2,4,128]{3,0,1,2:T(8,128)} %pad_maximum_fusion.14), channel_id=1, source_target_pairs={{0,16},{16,0},{1,17},{17,1},{2,18},{18,2},{3,19},{19,3},{4,20},{20... | collective-permute-start | bytes 98312 | tf_op jit(solution)/shard_map/ppermute | solution.py:17
  242.4 1.2 copy-start.5
  243.6 1.8 copy-start.3
  244.5 1.0 copy-start.4
  245.4 1.1 slice-start.2
  246.6 1.2 slice-start
  247.8 1.4 slice-start.3
  (9 other events, 7.2 us)
where the time goes:
time: 252 us; the launch traced here: 251 us
  blocking collectives  115 us (46%)
  local copies, waits for them, and re-layouts  36.6 us (15%)
  matrix products  36.5 us (14%)
  starting transfers between devices  31.1 us (12%)
  other arithmetic  28.4 us (11%)
    psum x2, blocking collectives, per_device(): lax.psum((moments_local(direction_core, image_set), moments_local(image_s...  76.4 us
    psum x1, blocking collectives, per_device(): lax.psum(moments_local(start_core, start_core), ('grp', 'az', 'ax'))  38.6 us
    dot_general x14, matrix products, products(): jnp.einsum('vrax,wrax->vw', first_set, second_set, precision=exact_mode)  15.5 us
    ppermute x6, starting transfers between devices, extended(): before = lax.ppermute(last, axis, up)  13.6 us
    unnamed x50, local copies, waits for them, and re-layouts  12 us
    ppermute x6, starting transfers between devices, extended(): after = lax.ppermute(first, axis, down)  11.4 us
    dot_general x8, matrix products, combine(): return jnp.einsum('vrax,vw->wrax', vector_set, mixing, precision=exact_mode)  9.04 us
    dot_general x3, matrix products, column_part(): jnp.einsum('rs,vsc->vrc', matrix, flat_set, precision=exact_mode)  8.66 us
  transfers between devices with their start and end apart: 15, of which 2 were waited for; matrix products, arithmetic and copies ran while one was open for 14% of the time, Pallas kernels for 0%

commit v1 on v0

--- a/solution.py
+++ b/solution.py
@@ -105,7 +105,7 @@
     direction = right_side
     solution = jnp.zeros_like(right_side)
     start_core = residual
-    norms_now = lax.psum(moments_local(start_core, start_core), ("grp", "az", "ax"))
+    norms_now = lax.psum(lax.psum(moments_local(start_core, start_core), ("az", "ax")), "grp")
     for sweep in range(ITERS):
         image_set = apply_shallow(direction, matrix, diagonal_own, wet_area, layout)
         direction_core = direction

time: 252 us -> 289 us (1.15)
  blocking collectives: 115 us -> 151 us
    psum x2 -> x3, blocking collectives: 76.4 us -> 114 us  [per_device(): lax.psum((moments_local(direction_core, image_set), moments_local(image_s...]
    psum x1 -> x2, blocking collectives: 38.6 us -> 36.2 us  [the longest x1 31.3 us: per_device(): lax.psum(moments_local(start_core, start_core), ('az', 'ax'))]
    unnamed x50 -> x54, local copies, waits for them, and re-layouts: 12 us -> 12.8 us
  transfers between devices with their start and end apart: 15 -> 15, of which waited for: 2 -> 2; matrix products, arithmetic and copies ran while one was open for 14% -> 13% of each run, Pallas kernels for 0% -> 0%
where the time goes in v1:
time: 289 us; the launch traced here: 287 us
  blocking collectives  151 us (52%)
  local copies, waits for them, and re-layouts  37.6 us (13%)
  matrix products  35.8 us (12%)
  starting transfers between devices  31.2 us (11%)
  other arithmetic  28.9 us (10%)
    psum x3, blocking collectives, per_device(): lax.psum((moments_local(direction_core, image_set), moments_local(image_s...  114 us
    psum x1, blocking collectives, per_device(): lax.psum(moments_local(start_core, start_core), ('az', 'ax'))  31.3 us
    dot_general x14, matrix products, products(): jnp.einsum('vrax,wrax->vw', first_set, second_set, precision=exact_mode)  14.9 us
    ppermute x6, starting transfers between devices, extended(): before = lax.ppermute(last, axis, up)  13.6 us
    unnamed x54, local copies, waits for them, and re-layouts  12.8 us
    ppermute x6, starting transfers between devices, extended(): after = lax.ppermute(first, axis, down)  11.5 us
    dot_general x8, matrix products, combine(): return jnp.einsum('vrax,vw->wrax', vector_set, mixing, precision=exact_mode)  9.06 us
    dot_general x3, matrix products, column_part(): jnp.einsum('rs,vsc->vrc', matrix, flat_set, precision=exact_mode)  8.66 us
  transfers between devices with their start and end apart: 15, of which 2 were waited for; matrix products, arithmetic and copies ran while one was open for 13% of the time, Pallas kernels for 0%

profile of v1, /device:TPU:0, one launch (start us, length us, event | category | flops | bytes accessed | tf_op | source)
XLA Modules:
  0.0 287.2 jit_solution(8119723324928239516)
XLA Ops:
  0.6 2.5 fusion.124
  5.1 2.4 collective-permute-start.3
  9.2 2.4 collective-permute-start.1
  11.6 3.1 %collective-permute-start = (f32[8,54,1,128]{3,0,1,2:T(8,128)S(1)}, f32[8,54,1,128]{3,0,1,2:T(8,128)}, u32[]{:S(2)}, u32[]{:S(2)}) collective-permute-start(f32[8,54,1,128]{3,0,1,2:T(8,128)S(1)} %get-tuple-element.109), channel_id=1, source_target_pairs={{2,0},{4,2},{6,4},{8,6},{10,8},{12,10},{14,12},{0,14},{3,1},{5,3},... | collective-permute-start | bytes 663560 | tf_op jit(solution)/shard_map/ppermute | solution.py:28
  17.7 1.9 convolution_bitcast_fusion.3
  20.0 31.3 %psum.64 = f32[8,8]{0,1:T(8,128)S(1)} all-reduce(f32[8,8]{0,1:T(8,128)S(1)} %fusion.13), channel_id=1, replica_groups=mesh['grp'=2,'az'=8,'ax'=2] {'az','ax'}, use_global_device_ids=true, to_apply=%region_3.0 | all-reduce | flops 64 | bytes 512 | tf_op jit(solution)/shard_map/psum | solution.py:108
  51.2 4.9 %psum.65 = f32[8,8]{0,1:T(8,128)S(1)} all-reduce(f32[8,8]{0,1:T(8,128)S(1)} %psum.64), channel_id=1, replica_groups=mesh['grp'=2,'az'=8,'ax'=2] {'grp'}, use_global_device_ids=true, to_apply=%region_4.0 | all-reduce | flops 64 | bytes 512 | tf_op jit(solution)/shard_map/psum | solution.py:108
  58.5 2.4 convolution_bitcast_fusion.2
  66.3 2.3 fusion.26
  70.8 1.9 convolution_bitcast_fusion.15
  75.1 37.2 %all-reduce.3 = (f32[8,8]{1,0:T(8,128)S(1)}, f32[8,8]{0,1:T(8,128)S(1)}, f32[8,8]{0,1:T(8,128)S(1)}) all-reduce(f32[8,8]{1,0:T(8,128)S(1)} %bitcast.241, f32[8,8]{0,1:T(8,128)S(1)} %fusion.11, f32[8,8]{0,1:T(8,128)S(1)} %fusion.9), channel_id=1, replica_groups=mesh['grp'=2,'az'=8,'ax'=2] {'grp','az','ax'}, use_global_device_ids=true, to_apply=%region_0.1 | all-reduce | flops 192 | bytes 1536 | tf_op jit(solution)/shard_map/psum | solution.py:113
  115.5 1.9 fusion.31
  124.2 2.1 copy.206
  126.3 1.9 collective-permute-start.8
  130.5 2.3 collective-permute-start.6
  132.8 2.4 collective-permute-start.5
  135.2 3.1 %convolution_bitcast_fusion.1 = f32[8,54,512]{2,1,0:T(8,128)} fusion(f32[8,54,512]{2,0,1:T(8,128)S(1)} %bitcast.235, f32[6,6]{1,0:T(8,128)S(1)} %copy-done.16, f32[48,48]{1,0:T(8,128)} %bitcast.238), kind=kOutput, calls=%fused_computation.1 | convolution fusion | flops 143341808 | bytes 1778832 | tf_op jit(solution)/shard_map/rs,vsc->vrc/dot_general | solution.py:49
  139.0 2.3 collective-permute-start.9
  147.7 2.5 fusion.22
  151.7 1.8 convolution_bitcast_fusion.11
  153.5 1.8 convolution_bitcast_fusion.9
  158.0 39.1 %all-reduce.2 = (f32[8,8]{0,1:T(8,128)S(1)}, f32[8,8]{0,1:T(8,128)}, f32[8,8]{0,1:T(8,128)}) all-reduce(f32[8,8]{0,1:T(8,128)S(1)} %fusion.7, f32[8,8]{0,1:T(8,128)S(1)} %fusion.5, f32[8,8]{0,1:T(8,128)S(1)} %fusion.3), channel_id=1, replica_groups=mesh['grp'=2,'az'=8,'ax'=2] {'grp','az','ax'}, use_global_device_ids=true, to_apply=%region_7.11 | all-reduce | flops 192 | bytes 1536 | tf_op jit(solution)/shard_map/psum | solution.py:113
  207.5 1.9 convolution_add_fusion.2
  209.3 2.2 copy.237
  211.6 2.0 collective-permute-start.13
  215.8 2.7 collective-permute-start.11
  218.5 2.1 collective-permute-start.10
  220.6 3.1 %convolution_bitcast_fusion = f32[8,54,512]{2,1,0:T(8,128)} fusion(f32[8,54,512]{2,0,1:T(8,128)S(1)} %bitcast.236, f32[6,6]{1,0:T(8,128)S(1)} %copy-done.16, f32[48,48]{1,0:T(8,128)} %bitcast.239), kind=kOutput, calls=%fused_computation | convolution fusion | flops 143341808 | bytes 1778832 | tf_op jit(solution)/shard_map/rs,vsc->vrc/dot_general | solution.py:49
  224.3 2.2 collective-permute-start.14
  229.9 1.8 collective-permute-done.10
  231.7 2.4 fusion.18
  237.7 38.0 %psum.71 = f32[8,8]{0,1:T(8,128)S(1)} all-reduce(f32[8,8]{0,1:T(8,128)S(1)} %fusion.1), channel_id=1, replica_groups=mesh['grp'=2,'az'=8,'ax'=2] {'grp','az','ax'}, use_global_device_ids=true, to_apply=%region_10.14 | all-reduce | flops 64 | bytes 512 | tf_op jit(solution)/shard_map/psum | solution.py:113
  (187 shorter events, 74.1 us)
Async XLA Ops:
  0.6 2.5 copy-start.7
  5.1 57.7 %collective-permute-start.3 = (f32[8,54,4,1]{1,0,3,2:T(8,128)}, f32[8,54,4,1]{1,0,3,2:T(8,128)S(1)}, u32[]{:S(2)}, u32[]{:S(2)}) collective-permute-start(f32[8,54,4,1]{1,0,3,2:T(8,128)} %copy.166), channel_id=1, source_target_pairs={{0,1},{2,3},{4,5},{6,7},{8,9},{10,11},{12,13},{14,15},{16,17},{18,... | collective-permute-start | bytes 20744 | tf_op jit(solution)/shard_map/ppermute | solution.py:27
  7.5 10.2 %copy-start = (f32[8,48,4,128]{3,2,1,0:T(4,128)S(1)}, f32[8,48,4,128]{3,2,1,0:T(4,128)}, u32[]{:S(2)}) copy-start(f32[8,48,4,128]{3,2,1,0:T(4,128)} %param.24) | copy-start | bytes 2359300
  7.9 56.3 %collective-permute-start.2 = (f32[8,54,4,1]{1,0,3,2:T(8,128)S(1)}, f32[8,54,4,1]{1,0,3,2:T(8,128)S(1)}, u32[]{:S(2)}, u32[]{:S(2)}) collective-permute-start(f32[8,54,4,1]{1,0,3,2:T(8,128)S(1)} %copy.164), channel_id=1, source_target_pairs={{1,0},{3,2},{5,4},{7,6},{9,8},{11,10},{13,12},{15,14},{17,16},{19,... | collective-permute-start | bytes 20744 | tf_op jit(solution)/shard_map/ppermute | solution.py:28
  9.2 56.4 %collective-permute-start.1 = (f32[8,54,1,128]{3,0,1,2:T(8,128)S(1)}, f32[8,54,1,128]{3,0,1,2:T(8,128)S(1)}, u32[]{:S(2)}, u32[]{:S(2)}) collective-permute-start(f32[8,54,1,128]{3,0,1,2:T(8,128)S(1)} %get-tuple-element.110), channel_id=1, source_target_pairs={{0,2},{2,4},{4,6},{6,8},{8,10},{10,12},{12,14},{14,0},{1,3},{3,5},... | collective-permute-start | bytes 663560 | tf_op jit(solution)/shard_map/ppermute | solution.py:27
  11.6 54.7 %collective-permute-start = (f32[8,54,1,128]{3,0,1,2:T(8,128)S(1)}, f32[8,54,1,128]{3,0,1,2:T(8,128)}, u32[]{:S(2)}, u32[]{:S(2)}) collective-permute-start(f32[8,54,1,128]{3,0,1,2:T(8,128)S(1)} %get-tuple-element.109), channel_id=1, source_target_pairs={{2,0},{4,2},{6,4},{8,6},{10,8},{12,10},{14,12},{0,14},{3,1},{5,3},... | collective-permute-start | bytes 663560 | tf_op jit(solution)/shard_map/ppermute | solution.py:28
  16.1 52.5 %collective-permute-start.4 = (f32[8,2,4,128]{3,0,1,2:T(8,128)}, f32[8,2,4,128]{3,0,1,2:T(8,128)}, u32[]{:S(2)}, u32[]{:S(2)}) collective-permute-start(f32[8,2,4,128]{3,0,1,2:T(8,128)} %pad_maximum_fusion.12), channel_id=1, source_target_pairs={{0,16},{16,0},{1,17},{17,1},{2,18},{18,2},{3,19},{19,3},{4,20},{20... | collective-permute-start | bytes 98312 | tf_op jit(solution)/shard_map/ppermute | solution.py:17
  51.2 7.2 %copy-start.9 = (f32[1,48,48]{2,1,0:T(8,128)S(1)}, f32[1,48,48]{2,1,0:T(8,128)}, u32[]{:S(2)}) copy-start(f32[1,48,48]{2,1,0:T(8,128)} %param.26) | copy-start | bytes 27652
  58.5 2.4 copy-start.23
  58.5 2.4 copy-start.13
  58.5 2.4 copy-start.21
  61.6 4.7 %copy-start.1 = (f32[8,54,512]{2,1,0:T(8,128)S(1)}, f32[8,54,512]{2,1,0:T(8,128)}, u32[]{:S(2)}) copy-start(f32[8,54,512]{2,1,0:T(8,128)} %convolution_bitcast_fusion.2) | copy-start | bytes 2654212
  72.7 1.8 copy-start.8
  126.3 18.3 %collective-permute-start.8 = (f32[8,54,4,1]{1,0,3,2:T(8,128)}, f32[8,54,4,1]{1,0,3,2:T(8,128)}, u32[]{:S(2)}, u32[]{:S(2)}) collective-permute-start(f32[8,54,4,1]{1,0,3,2:T(8,128)} %copy.206), channel_id=1, source_target_pairs={{0,1},{2,3},{4,5},{6,7},{8,9},{10,11},{12,13},{14,15},{16,17},{18,... | collective-permute-start | bytes 20744 | tf_op jit(solution)/shard_map/ppermute | solution.py:27
  129.2 16.5 %collective-permute-start.7 = (f32[8,54,4,1]{1,0,3,2:T(8,128)}, f32[8,54,4,1]{1,0,3,2:T(8,128)S(1)}, u32[]{:S(2)}, u32[]{:S(2)}) collective-permute-start(f32[8,54,4,1]{1,0,3,2:T(8,128)} %copy.204), channel_id=1, source_target_pairs={{1,0},{3,2},{5,4},{7,6},{9,8},{11,10},{13,12},{15,14},{17,16},{19,... | collective-permute-start | bytes 20744 | tf_op jit(solution)/shard_map/ppermute | solution.py:28
  130.5 16.6 %collective-permute-start.6 = (f32[8,54,1,128]{3,0,1,2:T(8,128)}, f32[8,54,1,128]{3,0,1,2:T(8,128)S(1)}, u32[]{:S(2)}, u32[]{:S(2)}) collective-permute-start(f32[8,54,1,128]{3,0,1,2:T(8,128)} %get-tuple-element.106), channel_id=1, source_target_pairs={{0,2},{2,4},{4,6},{6,8},{8,10},{10,12},{12,14},{14,0},{1,3},{3,5},... | collective-permute-start | bytes 663560 | tf_op jit(solution)/shard_map/ppermute | solution.py:27
  132.8 14.9 %collective-permute-start.5 = (f32[8,54,1,128]{3,0,1,2:T(8,128)}, f32[8,54,1,128]{3,0,1,2:T(8,128)}, u32[]{:S(2)}, u32[]{:S(2)}) collective-permute-start(f32[8,54,1,128]{3,0,1,2:T(8,128)} %get-tuple-element.105), channel_id=1, source_target_pairs={{2,0},{4,2},{6,4},{8,6},{10,8},{12,10},{14,12},{0,14},{3,1},{5,3},... | collective-permute-start | bytes 663560 | tf_op jit(solution)/shard_map/ppermute | solution.py:28
  135.2 3.1 %copy-start.14 = (f32[8,1,4,128]{3,0,1,2:T(8,128)S(1)}, f32[8,1,4,128]{3,0,1,2:T(8,128)}, u32[]{:S(2)}) copy-start(f32[8,1,4,128]{3,0,1,2:T(8,128)} %get-tuple-element.103) | copy-start | bytes 49156
  135.2 3.1 %copy-start.15 = (f32[8,1,4,128]{3,0,1,2:T(8,128)S(1)}, f32[8,1,4,128]{3,0,1,2:T(8,128)}, u32[]{:S(2)}) copy-start(f32[8,1,4,128]{3,0,1,2:T(8,128)} %get-tuple-element.104) | copy-start | bytes 49156
  138.4 2.9 %copy-start.19 = (f32[8,8]{1,0:T(8,128)S(1)}, f32[8,8]{1,0:T(8,128)}, u32[]{:S(2)}) copy-start(f32[8,8]{1,0:T(8,128)} %copy.218) | copy-start | bytes 772
  139.0 11.2 %collective-permute-start.9 = (f32[8,2,4,128]{3,0,1,2:T(8,128)}, f32[8,2,4,128]{3,0,1,2:T(8,128)}, u32[]{:S(2)}, u32[]{:S(2)}) collective-permute-start(f32[8,2,4,128]{3,0,1,2:T(8,128)} %pad_maximum_fusion.13), channel_id=1, source_target_pairs={{0,16},{16,0},{1,17},{17,1},{2,18},{18,2},{3,19},{19,3},{4,20},{20... | collective-permute-start | bytes 98312 | tf_op jit(solution)/shard_map/ppermute | solution.py:17
  206.3 1.2 copy-start.3
  209.3 4.2 %copy-start.2 = (f32[8,54,4,1]{3,0,1,2:T(8,128)S(1)}, f32[8,54,4,1]{3,0,1,2:T(8,128)}, u32[]{:S(2)}) copy-start(f32[8,54,4,1]{3,0,1,2:T(8,128)} %get-tuple-element.101) | copy-start | bytes 20740
  211.6 15.0 %collective-permute-start.13 = (f32[8,54,4,1]{1,0,3,2:T(8,128)}, f32[8,54,4,1]{1,0,3,2:T(8,128)}, u32[]{:S(2)}, u32[]{:S(2)}) collective-permute-start(f32[8,54,4,1]{1,0,3,2:T(8,128)} %copy.237), channel_id=1, source_target_pairs={{0,1},{2,3},{4,5},{6,7},{8,9},{10,11},{12,13},{14,15},{16,17},{18,... | collective-permute-start | bytes 20744 | tf_op jit(solution)/shard_map/ppermute | solution.py:27
  214.5 13.2 %collective-permute-start.12 = (f32[8,54,4,1]{1,0,3,2:T(8,128)}, f32[8,54,4,1]{1,0,3,2:T(8,128)S(1)}, u32[]{:S(2)}, u32[]{:S(2)}) collective-permute-start(f32[8,54,4,1]{1,0,3,2:T(8,128)} %copy.235), channel_id=1, source_target_pairs={{1,0},{3,2},{5,4},{7,6},{9,8},{11,10},{13,12},{15,14},{17,16},{19,... | collective-permute-start | bytes 20744 | tf_op jit(solution)/shard_map/ppermute | solution.py:28
  215.8 13.4 %collective-permute-start.11 = (f32[8,54,1,128]{3,0,1,2:T(8,128)}, f32[8,54,1,128]{3,0,1,2:T(8,128)S(1)}, u32[]{:S(2)}, u32[]{:S(2)}) collective-permute-start(f32[8,54,1,128]{3,0,1,2:T(8,128)} %get-tuple-element.100), channel_id=1, source_target_pairs={{0,2},{2,4},{4,6},{6,8},{8,10},{10,12},{12,14},{14,0},{1,3},{3,5},... | collective-permute-start | bytes 663560 | tf_op jit(solution)/shard_map/ppermute | solution.py:27
  218.5 13.2 %collective-permute-start.10 = (f32[8,54,1,128]{3,0,1,2:T(8,128)}, f32[8,54,1,128]{3,0,1,2:T(8,128)}, u32[]{:S(2)}, u32[]{:S(2)}) collective-permute-start(f32[8,54,1,128]{3,0,1,2:T(8,128)} %get-tuple-element.99), channel_id=1, source_target_pairs={{2,0},{4,2},{6,4},{8,6},{10,8},{12,10},{14,12},{0,14},{3,1},{5,3},... | collective-permute-start | bytes 663560 | tf_op jit(solution)/shard_map/ppermute | solution.py:28
  224.3 9.9 %collective-permute-start.14 = (f32[8,2,4,128]{3,0,1,2:T(8,128)}, f32[8,2,4,128]{3,0,1,2:T(8,128)}, u32[]{:S(2)}, u32[]{:S(2)}) collective-permute-start(f32[8,2,4,128]{3,0,1,2:T(8,128)} %pad_maximum_fusion.14), channel_id=1, source_target_pairs={{0,16},{16,0},{1,17},{17,1},{2,18},{18,2},{3,19},{19,3},{4,20},{20... | collective-permute-start | bytes 98312 | tf_op jit(solution)/shard_map/ppermute | solution.py:17
  278.9 1.2 copy-start.6
  280.1 1.8 copy-start.4
  283.0 1.2 slice-start
  284.2 1.4 slice-start.3
  (11 other events, 8.8 us)
